TPU v7x, 32 devices: a whole 2x2x4 slice. The times are simulated.
32 devices in a mesh: groups: 2 (over y), docs: 4 (over z), mp: 2 (over x), sub: 2 (over core).
Axes of the slice: x: 2, y: 2, z: 4, core: 2. Of those that a mesh axis runs over, the one named last changes fastest.
Arguments:
- embeddings: bfloat16 [4096, 1024], P(('groups', 'docs', 'mp', 'sub')), parts along dimension 0, may hold values from -6 to 6
- owner_shard: int32 [4096, 1], P(('groups', 'docs', 'mp', 'sub')), parts along dimension 0, may hold values from 0 to 3; in each aligned block of 128 rows (0 to 127, 128 to 255, ...) at most 64 rows name the same one
- query_local: int32 [4096], P(('groups', 'docs', 'mp', 'sub')), parts along dimension 0, may hold values from 0 to 1
- labels: int32 [4096], P(('groups', 'docs', 'mp', 'sub')), parts along dimension 0, may hold values from 0 to 4
- w_first: bfloat16 [1024, 1024], replicated, may hold values from -0.1875 to 0.1875
- w_second: float32 [1024], replicated, may hold values from -0.1875 to 0.1875
Outputs:
- emb_grad: bfloat16 [4096, 1024], P(('groups', 'docs', 'mp', 'sub')), parts along dimension 0
- w_first_grad: float32 [2048, 1024], P(('groups', 'mp', 'sub')), parts along dimension 0
- w_second_grad: float32 [2048], P('groups'), parts along dimension 0
There are 2 independent parts, one for each index of `groups`. A program takes and returns all parts, laid end to end along the dimension named above; an argument that names none is the same for every part. Nothing has to cross between parts.
Inputs may be any that keep to these rules, and one draw needn't show every extreme that they name: `owner_shard`: among the 128 rows of one document shard no owner appears more than 64 times, and some owner appears exactly 64 times.
All inputs are finite; a program needn't handle non-finite values.
Results may differ from a plain program's by a relative error of at most 0.017.
Values may be sent and summed in bfloat16 or wider, within the bound.
A program may use at most 64 MiB of HBM per device.

v0:
```python
import functools

import jax
import jax.numpy as jnp
from jax import lax
from jax.experimental import pallas as pl
from jax.experimental.pallas import tpu as pltpu
from jax.sharding import PartitionSpec as P

MESH = pl.DeviceIdType.MESH
LANES = 128
LOG2E = 1.4426950408889634


def log2(v):
    return jnp.log(v) * LOG2E


def across(row, rows):
    return jnp.broadcast_to(row, (rows, row.shape[1])).T


def row_tile(column):
    return jnp.broadcast_to(column, (column.shape[0], LANES)).T[0:8, :]


def kernel(
    sizes,
    emb_hbm, w1_hbm, owner_ref, local_ref, labels_ref, w2_ref,
    emb_grad_ref, w1g_ref, w2g_ref,
    w1v, embs, slope, hid, pg, at, wacc,
    minfo, sinfo, term, drow, lam, w2p,
    part, from_out, from_in, tot,
    load_sem, emb_send, emb_recv, m_send, m_recv, s_send, s_recv,
    l_send, l_recv, g_send, g_recv, in_send, out_send, fo_recv, fi_recv,
):
    D, M, S, C, E, H, rows, Kc, Kr = sizes
    L = M * S
    K = Kc * Kr
    d, m, s = lax.axis_index("docs"), lax.axis_index("mp"), lax.axis_index("sub")
    me = m * S + s

    load_w = pltpu.make_async_copy(w1_hbm, w1v, load_sem.at[0])
    load_e = pltpu.make_async_copy(emb_hbm, embs.at[pl.ds(me * C, C)], load_sem.at[1])
    load_e.start()
    load_w.start()

    def doc_peer(k):
        return lax.rem(d + k, D)

    def mp_peer(k):
        return lax.rem(m + k, M)

    def sub_peer(k):
        return lax.rem(s + k, S)

    lane_steps = [(a, b) for a in range(M) for b in range(S) if a or b]

    barrier = pltpu.get_barrier_semaphore()
    for k in range(1, D):
        pl.semaphore_signal(barrier, inc=1, device_id={"docs": doc_peer(k)}, device_id_type=MESH)
    for a, b in lane_steps:
        pl.semaphore_signal(
            barrier, inc=1, device_id={"mp": mp_peer(a), "sub": sub_peer(b)}, device_id_type=MESH
        )

    lab_own = labels_ref[...].astype(jnp.float32)
    q_own = (owner_ref[...] * 1024 + local_ref[...]).astype(jnp.float32)
    minfo[d, 0:1, :] = lab_own
    minfo[d, 1:2, :] = q_own

    pl.semaphore_wait(barrier, D - 1 + L - 1)

    def doc_send(buf, k, send, recv):
        return pltpu.make_async_remote_copy(
            src_ref=buf.at[d], dst_ref=buf.at[d], send_sem=send.at[k], recv_sem=recv.at[k],
            device_id={"docs": doc_peer(k)}, device_id_type=MESH,
        )

    load_e.wait()

    def emb_copy(lane, a, b, index):
        block = embs.at[pl.ds(lane * C, C)]
        return pltpu.make_async_remote_copy(
            src_ref=block, dst_ref=block, send_sem=emb_send.at[index], recv_sem=emb_recv.at[index],
            device_id={"mp": mp_peer(a), "sub": sub_peer(b)}, device_id_type=MESH,
        )

    for a in range(1, M):
        emb_copy(me, a, 0, a * S).start()
    for b in range(1, S):
        emb_copy(me, 0, b, b).start()
    for k in range(1, D):
        doc_send(minfo, k, m_send, m_recv).start()

    w2 = w2_ref[...]

    def forward(lane):
        at_rows = pl.ds(lane * C, C)
        act = jnp.dot(embs[at_rows, :], w1v[...], preferred_element_type=jnp.float32)
        sg = jax.nn.sigmoid(act)
        hidden = act * sg
        hid[at_rows, :] = hidden
        slope[at_rows, :] = w2 * (sg * (1.0 + act * (1.0 - sg)))
        return hidden

    load_w.wait()
    hidden = forward(me)
    sinfo[d] = row_tile(jnp.sum(hidden * w2, axis=1, keepdims=True))
    for k in range(1, D):
        doc_send(sinfo, k, s_send, s_recv).start()

    def lane_from(a, b):
        return lax.rem(m + M - a, M) * S + lax.rem(s + S - b, S)

    def recv_wait(a, b):
        emb_copy(lane_from(a, b), a, b, a * S + b).wait_recv()

    for b in range(1, S):
        recv_wait(0, b)
        forward(lane_from(0, b))

    for k in range(1, D):
        doc_send(minfo, k, m_send, m_recv).wait_recv()
    slot = lax.broadcasted_iota(jnp.int32, (1, C), 1).astype(jnp.float32)
    total = float(D * C)

    def key_of(label_row, dd):
        return label_row * total - (slot + lax.convert_element_type(dd * C, jnp.float32))

    def ideal_step(jd, carry):
        q_j = across(minfo[jd, 1:2, :], C)
        key_j = across(key_of(minfo[jd, 0:1, :], jd), C)
        out = []
        for i in range(D):
            ahead = (q_j == minfo[i, 1:2, :]) & (key_j > key_of(minfo[i, 0:1, :], i))
            out.append(carry[i] + jnp.sum(jnp.where(ahead, 1.0, 0.0), axis=0, keepdims=True))
        return tuple(out)

    zeros = tuple(jnp.zeros((1, C), jnp.float32) for _ in range(D))
    ideal = lax.fori_loop(0, D, ideal_step, zeros)
    for i in range(D):
        gain = jnp.exp2(minfo[i, 0:1, :]) - 1.0
        term[i, 0:1, :] = gain / log2(2.0 + ideal[i])
    q_i = across(q_own, C)
    gain_i = across(jnp.exp2(lab_own) - 1.0, C)
    idcg = jnp.zeros((C, C), jnp.float32)
    for j in range(D):
        idcg = idcg + jnp.where(q_i == minfo[j, 1:2, :], term[j, 0:1, :], 0.0)
    idcg = jnp.sum(idcg, axis=1, keepdims=True)
    inv = jnp.where(idcg > 0.0, 1.0 / jnp.where(idcg > 0.0, idcg, 1.0), 0.0)

    for k in range(1, D):
        doc_send(sinfo, k, s_send, s_recv).wait_recv()

    def soft_step(jd, carry):
        q_j = across(minfo[jd, 1:2, :], C)
        s_j = across(sinfo[jd, 0:1, :], C)
        out = []
        for i in range(D):
            part_of = jnp.where(
                q_j == minfo[i, 1:2, :], jax.nn.sigmoid(s_j - sinfo[i, 0:1, :]), 0.0
            )
            out.append(carry[i] + jnp.sum(part_of, axis=0, keepdims=True))
        return tuple(out)

    soft = lax.fori_loop(0, D, soft_step, zeros)
    for i in range(D):
        drow[i, 0:1, :] = 1.0 / log2(2.0 + (soft[i] - 0.5))
    disc_i = across(drow[d, 0:1, :], C)
    s_i = across(sinfo[d, 0:1, :], C)

    def lambda_step(j, acc):
        gain_j = jnp.exp2(minfo[j, 0:1, :]) - 1.0
        gap = s_i - sinfo[j, 0:1, :]
        weight = (gain_j - gain_i) * jnp.abs(disc_i - drow[j, 0:1, :])
        push = jax.nn.sigmoid(jnp.where(gain_i > gain_j, -gap, gap))
        return acc + jnp.where(q_i == minfo[j, 1:2, :], weight * push, 0.0)

    lam_acc = lax.fori_loop(0, D, lambda_step, jnp.zeros((C, C), jnp.float32))
    lam_col = jnp.sum(lam_acc, axis=1, keepdims=True) * inv
    lam[me] = row_tile(lam_col)

    def lam_copy(lane, a, b):
        return pltpu.make_async_remote_copy(
            src_ref=lam.at[lane], dst_ref=lam.at[lane],
            send_sem=l_send.at[a * S + b], recv_sem=l_recv.at[a * S + b],
            device_id={"mp": mp_peer(a), "sub": sub_peer(b)}, device_id_type=MESH,
        )

    for a, b in lane_steps:
        lam_copy(me, a, b).start()

    def scale(lane, column):
        at_rows = pl.ds(lane * C, C)
        pg[at_rows, :] = (column * slope[at_rows, :]).astype(jnp.bfloat16)

    scale(me, lam_col)
    emb_grad_ref[...] = lax.dot_general(
        pg[pl.ds(me * C, C), :], w1v[...], (((1,), (1,)), ((), ())),
        preferred_element_type=jnp.float32,
    ).astype(jnp.bfloat16)
    for a in range(1, M):
        recv_wait(a, 0)
        for b in range(1, S):
            emb_copy(lane_from(a, 0), 0, b, a * S + b).start()
        forward(lane_from(a, 0))
    for a in range(1, M):
        for b in range(1, S):
            recv_wait(a, b)
            forward(lane_from(a, b))
    width = at.shape[0]
    first = pl.multiple_of((me * rows) // LANES * LANES, LANES)
    for lane in range(L):
        at[:, pl.ds(lane * C, C)] = embs[pl.ds(lane * C, C), pl.ds(first, width)].T

    for a, b in lane_steps:
        lam_copy(lane_from(a, b), a, b).wait_recv()
        lane = lane_from(a, b)
        scale(lane, across(lam[lane, 0:1, :], C)[:, 0:1])

    half = D // 2
    left = d < half
    inward = jnp.where(left, d + 1, d - 1)
    outward = jnp.where(left, d - 1, d + 1)
    place = jnp.where(left, d, D - 1 - d)
    has_out = place > 0
    middle = place == half - 1
    cw, rh = H // Kc, rows // Kr

    def send_in(k, to_middle):
        dst, sem = (from_in, fi_recv) if to_middle else (from_out, fo_recv)
        return pltpu.make_async_remote_copy(
            src_ref=part.at[k], dst_ref=dst.at[k], send_sem=in_send.at[k], recv_sem=sem.at[k],
            device_id={"docs": inward}, device_id_type=MESH,
        )

    def send_out(k, from_total):
        src = tot if from_total else from_in
        return pltpu.make_async_remote_copy(
            src_ref=src.at[k], dst_ref=from_in.at[k], send_sem=out_send.at[k],
            recv_sem=fi_recv.at[k], device_id={"docs": outward}, device_id_type=MESH,
        )

    def start_in(k):
        pl.when(middle)(lambda: send_in(k, True).start())
        if half > 1:
            pl.when(jnp.logical_not(middle))(lambda: send_in(k, False).start())

    shift = me * rows - first
    for c in range(Kc):
        wide = jnp.dot(at[...], pg[:, c * cw : (c + 1) * cw], preferred_element_type=jnp.float32)
        wacc[c] = wide
        for r in range(Kr):
            k = c * Kr + r

            @pl.when(jnp.logical_not(has_out))
            def _():
                part[k] = wacc[c, pl.ds(pl.multiple_of(shift + r * rh, 8), rh), :].astype(
                    jnp.bfloat16
                )
                start_in(k)

    w2_part = jnp.zeros((1, H), jnp.float32)
    for lane in range(L):
        column = across(lam[lane, 0:1, :], C)[:, 0:1]
        w2_part = w2_part + jnp.sum(column * hid[pl.ds(lane * C, C), :], axis=0, keepdims=True)
    for j in range(H // LANES):
        w2p[d, j : j + 1, :] = w2_part[:, j * LANES : (j + 1) * LANES]
    for k in range(1, D):
        doc_send(w2p, k, g_send, g_recv).start()

    def gather_step(k):
        c, r = k // Kr, k % Kr

        @pl.when(has_out)
        def _():
            send_in(k, False).wait_recv()
            own = wacc[c, pl.ds(pl.multiple_of(shift + r * rh, 8), rh), :]
            part[k] = (own + from_out[k].astype(jnp.float32)).astype(jnp.bfloat16)
            start_in(k)

    def finish_step(k):
        c, r = k // Kr, k % Kr
        send_out(k, False).wait_recv()
        spot = (slice(r * rh, (r + 1) * rh), slice(c * cw, (c + 1) * cw))

        @pl.when(middle)
        def _():
            both = (part[k].astype(jnp.float32) + from_in[k].astype(jnp.float32)).astype(
                jnp.bfloat16
            )
            w1g_ref[spot] = both.astype(jnp.float32)
            if half > 1:
                tot[k] = both
                pl.when(has_out)(lambda: send_out(k, True).start())

        if half > 1:

            @pl.when(jnp.logical_not(middle))
            def _():
                pl.when(has_out)(lambda: send_out(k, False).start())
                w1g_ref[spot] = from_in[k].astype(jnp.float32)

    lag = max(1, K // 4)
    for k in range(lag):
        gather_step(k)
    for k in range(lag, K + lag):
        if k < K:
            gather_step(k)
        finish_step(k - lag)

    for k in range(1, D):
        doc_send(w2p, k, g_send, g_recv).wait_recv()
    w2_sum = w2p[0]
    for j in range(1, D):
        w2_sum = w2_sum + w2p[j]
    for j in range(H // LANES):
        w2g_ref[0:1, j * LANES : (j + 1) * LANES] = w2_sum[j : j + 1, :]

    for k in range(1, D):
        doc_send(minfo, k, m_send, m_recv).wait_send()
        doc_send(sinfo, k, s_send, s_recv).wait_send()
        doc_send(w2p, k, g_send, g_recv).wait_send()
    for a, b in lane_steps:
        emb_copy(me, a, b, a * S + b).wait_send()
        lam_copy(me, a, b).wait_send()
    for k in range(K):
        send_in(k, True).wait_send()
    for k in range(K):
        pl.when(has_out)(lambda k=k: send_out(k, False).wait_send())


def write_out(a_ref, b_ref, c_ref, a_out, b_out, c_out, sem):
    pairs = ((b_ref, b_out), (a_ref, a_out), (c_ref, c_out))
    copies = [pltpu.make_async_copy(x, y, sem.at[i]) for i, (x, y) in enumerate(pairs)]
    for copy in copies:
        copy.start()
    for copy in copies:
        copy.wait()


def on_device(embeddings, owner_shard, query_local, labels, w_first, w_second):
    D, M, S = lax.axis_size("docs"), lax.axis_size("mp"), lax.axis_size("sub")
    C, E = embeddings.shape
    H = w_first.shape[1]
    L = M * S
    rows = E // L
    width = max(rows, LANES)
    Kc = 4
    Kr = max(1, rows // 32)
    K = Kc * Kr
    f32, bf16 = jnp.float32, jnp.bfloat16
    vmem = pl.BlockSpec(memory_space=pltpu.VMEM)
    hbm = pl.BlockSpec(memory_space=pl.ANY)
    dma = pltpu.SemaphoreType.DMA
    chunk = (K, rows // Kr, H // Kc)
    scratch = [
        pltpu.VMEM((E, H), bf16),
        pltpu.VMEM((L * C, E), bf16),
        pltpu.VMEM((L * C, H), f32),
        pltpu.VMEM((L * C, H), f32),
        pltpu.VMEM((L * C, H), bf16),
        pltpu.VMEM((width, L * C), bf16),
        pltpu.VMEM((Kc, width, H // Kc), f32),
        pltpu.VMEM((D, 8, C), f32),
        pltpu.VMEM((D, 8, C), f32),
        pltpu.VMEM((D, 8, C), f32),
        pltpu.VMEM((D, 8, C), f32),
        pltpu.VMEM((L, 8, C), f32),
        pltpu.VMEM((D, H // LANES, LANES), f32),
        pltpu.VMEM(chunk, bf16),
        pltpu.VMEM(chunk, bf16),
        pltpu.VMEM(chunk, bf16),
        pltpu.VMEM(chunk, bf16),
        dma((2,)),
        dma((L,)), dma((L,)),
        dma((D,)), dma((D,)),
        dma((D,)), dma((D,)),
        dma((L,)), dma((L,)),
        dma((D,)), dma((D,)),
        dma((K,)), dma((K,)), dma((K,)), dma((K,)),
    ]
    emb_grad, w1g, w2g = pl.pallas_call(
        functools.partial(kernel, (D, M, S, C, E, H, rows, Kc, Kr)),
        out_shape=(
            pltpu.VMEM((C, E), bf16),
            pltpu.VMEM((rows, H), f32),
            pltpu.VMEM((1, H), f32),
        ),
        in_specs=[hbm, hbm, vmem, vmem, vmem, vmem],
        out_specs=(vmem, vmem, vmem),
        scratch_shapes=scratch,
        compiler_params=pltpu.CompilerParams(
            collective_id=0, has_side_effects=True, vmem_limit_bytes=56 * 1024 * 1024
        ),
    )(
        embeddings, w_first, owner_shard.reshape(1, C), query_local.reshape(1, C),
        labels.reshape(1, C), w_second.reshape(1, H),
    )
    emb_grad, w1g, w2g = pl.pallas_call(
        write_out,
        out_shape=tuple(jax.ShapeDtypeStruct(v.shape, v.dtype) for v in (emb_grad, w1g, w2g)),
        in_specs=[vmem] * 3,
        out_specs=(hbm,) * 3,
        scratch_shapes=[dma((3,))],
        compiler_params=pltpu.CompilerParams(vmem_limit_bytes=4 * 1024 * 1024),
    )(emb_grad, w1g, w2g)
    return emb_grad, w1g, w2g.reshape(H)


def solution(mesh):
    return jax.shard_map(
        on_device,
        mesh=mesh,
        in_specs=(
            P(("groups", "docs", "mp", "sub"), None),
            P(("groups", "docs", "mp", "sub"), None),
            P(("groups", "docs", "mp", "sub")),
            P(("groups", "docs", "mp", "sub")),
            P(),
            P(),
        ),
        out_specs=(
            P(("groups", "docs", "mp", "sub"), None),
            P(("groups", "mp", "sub"), None),
            P("groups"),
        ),
        check_vma=False,
    )
```

profile of v0, /device:TPU:0, one launch (start us, length us, event | category | flops | bytes accessed | tf_op | source)
XLA Modules:
  0.0 37.9 jit_solution(6274607791621685736)
XLA Ops:
  0.6 36.1 %shard_map.85 = (bf16[128,1024]{1,0:T(8,128)(2,1)S(1)}, f32[256,1024]{1,0:T(8,128)S(1)}, f32[1,1024]{1,0:T(1,128)S(1)}) custom-call(bf16[128,1024]{1,0:T(8,128)(2,1)} %emb_hbm.1, bf16[1024,1024]{1,0:T(8,128)(2,1)} %w1_hbm.1, s32[1,128]{1,0:T(1,128)} %bitcast.6, s32[1,128]{1,0:T(1,128)} %bitcast.7, s32[1,128]{1,0:T(1,128)} %bitcast.8, f32[1,1024]{1,0:T(1,128)} %bitcast.5), custom_call_target="tpu_custom_call" | custom-call | tf_op jit(solution)/shard_map/pallas_call | solution.py:384
  36.8 1.1 %shard_map.86 = (bf16[128,1024]{1,0:T(8,128)(2,1)}, f32[256,1024]{1,0:T(8,128)}, f32[1,1024]{1,0:T(1,128)}) custom-call(bf16[128,1024]{1,0:T(8,128)(2,1)S(1)} %get-tuple-element.9.a_ref, f32[256,1024]{1,0:T(8,128)S(1)} %get-tuple-element.10.b_ref, f32[1,1024]{1,0:T(1,128)S(1)} %get-tuple-element.11.c_ref), custom_call_target="tpu_custom_call" | custom-call | tf_op jit(solution)/shard_map/pallas_call | solution.py:401
where the time goes:
time: 38.1 us; the launch traced here: 37.9 us
  Pallas kernels  37.2 us (98%)
  between operations  0.64 us (2%)
    pallas_call x1, Pallas kernels, on_device(): pl.pallas_call(functools.partial(kernel, (D, M, S, C, E, H, rows, Kc, Kr)...  36.1 us
    pallas_call x1, Pallas kernels, on_device(): pl.pallas_call(write_out, out_shape=tuple((jax.ShapeDtypeStruct(v.shape,...  1.08 us

commit v1 on v0

--- a/solution.py
+++ b/solution.py
@@ -312,9 +312,9 @@
 
     for k in range(1, D):
         doc_send(w2p, k, g_send, g_recv).wait_recv()
-    w2_sum = w2p[0]
-    for j in range(1, D):
-        w2_sum = w2_sum + w2p[j]
+    w2_sum = w2p[d]
+    for k in range(1, D):
+        w2_sum = w2_sum + w2p[doc_peer(k)]
     for j in range(H // LANES):
         w2g_ref[0:1, j * LANES : (j + 1) * LANES] = w2_sum[j : j + 1, :]
 

time: 38.1 us -> 38.1 us (level)
  no operation moved by 1% of the time
where the time goes in v1:
time: 38.1 us; the launch traced here: 37.9 us
  Pallas kernels  37.2 us (98%)
  between operations  0.64 us (2%)
    pallas_call x1, Pallas kernels, on_device(): pl.pallas_call(functools.partial(kernel, (D, M, S, C, E, H, rows, Kc, Kr)...  36.1 us
    pallas_call x1, Pallas kernels, on_device(): pl.pallas_call(write_out, out_shape=tuple((jax.ShapeDtypeStruct(v.shape,...  1.08 us

profile of v1, /device:TPU:0, one launch (start us, length us, event | category | flops | bytes accessed | tf_op | source)
XLA Modules:
  0.0 37.9 jit_solution(6936060893717443338)
XLA Ops:
  0.6 36.1 %shard_map.85 = (bf16[128,1024]{1,0:T(8,128)(2,1)S(1)}, f32[256,1024]{1,0:T(8,128)S(1)}, f32[1,1024]{1,0:T(1,128)S(1)}) custom-call(bf16[128,1024]{1,0:T(8,128)(2,1)} %emb_hbm.1, bf16[1024,1024]{1,0:T(8,128)(2,1)} %w1_hbm.1, s32[1,128]{1,0:T(1,128)} %bitcast.6, s32[1,128]{1,0:T(1,128)} %bitcast.7, s32[1,128]{1,0:T(1,128)} %bitcast.8, f32[1,1024]{1,0:T(1,128)} %bitcast.5), custom_call_target="tpu_custom_call" | custom-call | tf_op jit(solution)/shard_map/pallas_call | solution.py:384
  36.8 1.1 %shard_map.86 = (bf16[128,1024]{1,0:T(8,128)(2,1)}, f32[256,1024]{1,0:T(8,128)}, f32[1,1024]{1,0:T(1,128)}) custom-call(bf16[128,1024]{1,0:T(8,128)(2,1)S(1)} %get-tuple-element.9.a_ref, f32[256,1024]{1,0:T(8,128)S(1)} %get-tuple-element.10.b_ref, f32[1,1024]{1,0:T(1,128)S(1)} %get-tuple-element.11.c_ref), custom_call_target="tpu_custom_call" | custom-call | tf_op jit(solution)/shard_map/pallas_call | solution.py:401

commit v2 on v0

--- a/solution.py
+++ b/solution.py
@@ -330,6 +330,384 @@
     for k in range(K):
         pl.when(has_out)(lambda k=k: send_out(k, False).wait_send())
 
+def ring_kernel(
+    sizes,
+    emb_hbm, w1_hbm, owner_hbm, local_hbm, labels_hbm, w2_hbm,
+    emb_grad_ref, w1g_ref, w2g_ref,
+    w1v, xs, slope, hid, small, w2v, pre, wtot,
+    info, term, drow, lam_all, lam_exp, lam_row, lam_pair,
+    load_sem, cw_send, cw_recv, ccw_send, ccw_recv, dd_send, dd_recv,
+    i_send, i_recv, l_send, l_recv, stage_sem,
+):
+    D, M, S, C, E, H, rows, P = sizes
+    N = D * M
+    PR = C // P
+    T = P * (N - 1) // 2
+    d, m, s = lax.axis_index("docs"), lax.axis_index("mp"), lax.axis_index("sub")
+    me = m * S + s
+    other = S - 1 - s
+    r = jnp.where(m == 0, d, N - 1 - d)
+
+    def ring_at(q):
+        q = lax.rem(q + 2 * N, N)
+        return {"docs": jnp.where(q < D, q, N - 1 - q), "mp": jnp.where(q < D, 0, 1)}
+
+    ahead_id, behind_id, twin_id = ring_at(r + 1), ring_at(r - 1), {"sub": other}
+
+    def spot(slot):
+        return lax.div(slot, 2), pl.multiple_of(lax.rem(slot, 2) * C, C)
+
+    def block(slot):
+        u, row = spot(slot)
+        return xs.at[u, pl.ds(row, C)]
+
+    load_e = pltpu.make_async_copy(emb_hbm, block(s), load_sem.at[0])
+    load_w = pltpu.make_async_copy(w1_hbm, w1v, load_sem.at[1])
+    load_small = [
+        pltpu.make_async_copy(owner_hbm, small.at[0], load_sem.at[2]),
+        pltpu.make_async_copy(local_hbm, small.at[1], load_sem.at[3]),
+        pltpu.make_async_copy(labels_hbm, small.at[2], load_sem.at[4]),
+        pltpu.make_async_copy(w2_hbm, w2v, load_sem.at[5]),
+    ]
+    barrier = pltpu.get_barrier_semaphore()
+    for peer in (ahead_id, behind_id, twin_id):
+        pl.semaphore_signal(barrier, inc=1, device_id=peer, device_id_type=MESH)
+    load_e.start()
+    load_w.start()
+    for copy in load_small:
+        copy.start()
+
+    def remote(src, dst, send, recv, peer):
+        return pltpu.make_async_remote_copy(
+            src_ref=src, dst_ref=dst, send_sem=send, recv_sem=recv,
+            device_id=peer, device_id_type=MESH,
+        )
+
+    def part(slot, lane_s, way):
+        return block(slot).at[pl.ds((lane_s * 2 + way) * PR, PR)]
+
+    def ahead_copy(src, t):
+        return remote(src, part(S + t, s, 0), cw_send.at[t], cw_recv.at[t], ahead_id)
+
+    def behind_copy(src, t):
+        return remote(src, part(S + t, s, 1), ccw_send.at[t], ccw_recv.at[t], behind_id)
+
+    def twin_copy(slot, lane_s):
+        both = block(slot).at[pl.ds(lane_s * 2 * PR, 2 * PR)]
+        return remote(both, both, dd_send.at[slot], dd_recv.at[slot], twin_id)
+
+    own_twin = remote(block(s), block(s), dd_send.at[0], dd_recv.at[0], twin_id)
+
+    def next_stage(k):
+        for peer in (ahead_id, behind_id):
+            pl.semaphore_signal(stage_sem.at[k], inc=1, device_id=peer, device_id_type=MESH)
+
+    def stage_wait(k):
+        pl.semaphore_wait(stage_sem.at[k], 2)
+
+    pl.semaphore_wait(barrier, 3)
+    load_e.wait()
+    def send_own(p):
+        ahead_copy(block(s).at[pl.ds(p * PR, PR)], p).start()
+        behind_copy(block(s).at[pl.ds((P - 1 - p) * PR, PR)], p).start()
+
+    for p in range(P // 2):
+        send_own(p)
+    own_twin.start()
+    stages = stage_sem.shape[0]
+    next_stage(0)
+
+    for copy in load_small:
+        copy.wait()
+    load_w.wait()
+    w2 = w2v[...]
+
+    def forward(slot):
+        u, row = spot(slot)
+        act = jnp.dot(xs[u, pl.ds(row, C), :], w1v[...], preferred_element_type=jnp.float32)
+        sg = 0.5 + 0.5 * jnp.tanh(0.5 * act)
+        hidden = act * sg
+        bend = sg + hidden * (1.0 - sg)
+        hid[u, pl.ds(row, C), :] = hidden.astype(jnp.bfloat16)
+        slope[u, pl.ds(row, C), :] = bend.astype(jnp.bfloat16)
+        return hidden, bend
+
+    hidden, bend = forward(s)
+    info[d] = row_tile(jnp.sum(hidden * w2, axis=1, keepdims=True))
+    info[d, 1:2, :] = small[2].astype(jnp.float32)
+    info[d, 2:3, :] = (small[0] * 1024 + small[1]).astype(jnp.float32)
+    stage_wait(0)
+    if stages > 1:
+        next_stage(1)
+    pre[...] = lax.dot_general(
+        (bend * w2).astype(jnp.bfloat16), w1v[...], (((1,), (1,)), ((), ())),
+        preferred_element_type=jnp.float32,
+    )
+    def doc_peer(k):
+        return lax.rem(d + k, D)
+
+    def info_copy(k):
+        return remote(
+            info.at[d], info.at[d], i_send.at[k], i_recv.at[k], {"docs": doc_peer(k)}
+        )
+
+    lane_steps = [(a, b) for a in range(M) for b in range(S) if a or b]
+
+    def lam_copy(a, b):
+        peer = {"mp": lax.rem(m + a, M), "sub": lax.rem(s + b, S)}
+        return remote(
+            lam_all.at[me], lam_all.at[me], l_send.at[a * S + b], l_recv.at[a * S + b], peer
+        )
+
+    reach = min(stages, max(1, D - 2))
+    for k in range(2, reach + 1):
+        stage_wait(k - 1)
+        if k < stages:
+            next_stage(k)
+    for k in range(1, D):
+        info_copy(k).start()
+    for p in range(P // 2, P):
+        send_own(p)
+    own_twin.wait_recv()
+    forward(other)
+
+    def relay(t):
+        ahead_copy(part(S + t, s, 0), t).wait_recv()
+
+        @pl.when(t + P < T)
+        def _():
+            ahead_copy(part(S + t, s, 0), t + P).start()
+
+        behind_copy(part(S + t, s, 1), t).wait_recv()
+
+        @pl.when(t + P < T)
+        def _():
+            behind_copy(part(S + t, s, 1), t + P).start()
+
+        twin_copy(S + t, s).start()
+
+    def step_forward(t):
+        twin_copy(S + t, other).wait_recv()
+        forward(S + t)
+
+    def relay_forward(lag, t, carry):
+        relay(t)
+        step_forward(t - lag)
+        return carry
+
+    early, late = T // 4 + 1, T // 2 + 1
+    relay(0)
+    lax.fori_loop(1, early, functools.partial(relay_forward, 1), 0)
+
+    for k in range(1, D):
+        info_copy(k).wait_recv()
+    slot_of = lax.broadcasted_iota(jnp.int32, (1, C), 1).astype(jnp.float32)
+    total = float(D * C)
+
+    def key_of(jd):
+        return info[jd, 1:2, :] * total - (slot_of + lax.convert_element_type(jd * C, jnp.float32))
+
+    def rank_step(jd, carry):
+        q_j = across(info[jd, 2:3, :], C)
+        s_j = across(info[jd, 0:1, :], C)
+        key_j = across(key_of(jd), C)
+        out = []
+        for i in range(D):
+            same = q_j == info[i, 2:3, :]
+            push = 0.5 + 0.5 * jnp.tanh(0.5 * (s_j - info[i, 0:1, :]))
+            ahead = same & (key_j > key_of(i))
+            out.append(carry[i] + jnp.sum(jnp.where(same, push, 0.0), axis=0, keepdims=True))
+            out.append(carry[D + i] + jnp.sum(jnp.where(ahead, 1.0, 0.0), axis=0, keepdims=True))
+        return tuple(out[0::2] + out[1::2])
+
+    zeros = tuple(jnp.zeros((1, C), jnp.float32) for _ in range(2 * D))
+    ranks = lax.fori_loop(0, D, rank_step, zeros)
+    for i in range(D):
+        gain = jnp.exp2(info[i, 1:2, :]) - 1.0
+        term[i, 0:1, :] = gain / log2(2.0 + ranks[D + i])
+        drow[i, 0:1, :] = 1.0 / log2(2.0 + (ranks[i] - 0.5))
+
+    relay(early)
+
+    def lambda_step(jd, carry):
+        q_j = across(info[jd, 2:3, :], C)
+        s_j = across(info[jd, 0:1, :], C)
+        gain_j = across(jnp.exp2(info[jd, 1:2, :]) - 1.0, C)
+        disc_j = across(drow[jd, 0:1, :], C)
+        term_j = across(term[jd, 0:1, :], C)
+        out = []
+        for i in range(D):
+            same = q_j == info[i, 2:3, :]
+            gain_i = jnp.exp2(info[i, 1:2, :]) - 1.0
+            gap = info[i, 0:1, :] - s_j
+            weight = (gain_j - gain_i) * jnp.abs(drow[i, 0:1, :] - disc_j)
+            push = 0.5 + 0.5 * jnp.tanh(0.5 * jnp.where(gain_i > gain_j, -gap, gap))
+            out.append(
+                carry[i] + jnp.sum(jnp.where(same, weight * push, 0.0), axis=0, keepdims=True)
+            )
+            out.append(
+                carry[D + i] + jnp.sum(jnp.where(same, term_j, 0.0), axis=0, keepdims=True)
+            )
+        return tuple(out[0::2] + out[1::2])
+
+    sums = lax.fori_loop(0, D, lambda_step, zeros)
+    for i in range(D):
+        idcg = sums[D + i]
+        inv = jnp.where(idcg > 0.0, 1.0 / jnp.where(idcg > 0.0, idcg, 1.0), 0.0)
+        lam_all[me, i : i + 1, :] = sums[i] * inv
+    for k in range(reach + 1, stages + 1):
+        stage_wait(k - 1)
+        if k < stages:
+            next_stage(k)
+    for a, b in lane_steps:
+        lam_copy(a, b).start()
+
+    for i in range(D):
+        lam_exp[me, i] = jnp.broadcast_to(lam_all[me, i : i + 1, :], (8, C))
+    emb_grad_ref[...] = (pre[...] * across(lam_exp[me, d, 0:1, :], C)[:, 0:1]).astype(jnp.bfloat16)
+
+    lax.fori_loop(early + 1, late, functools.partial(relay_forward, 2), 0)
+    step_forward(late - 2)
+
+    for a, b in lane_steps:
+        lam_copy(a, b).wait_recv()
+        lane = lax.rem(m + M - a, M) * S + lax.rem(s + S - b, S)
+        for i in range(D):
+            lam_exp[lane, i] = jnp.broadcast_to(lam_all[lane, i : i + 1, :], (8, C))
+
+    lane_no = lax.broadcasted_iota(jnp.int32, (8, C), 1) // PR
+    row_no = lax.broadcasted_iota(jnp.int32, (16, C), 0)
+
+    def put_lambda(slot, tile):
+        cols = slice(slot % 2 * C, slot % 2 * C + C)
+        lam_row[slot // 2, :, cols] = tile
+        high = tile.astype(jnp.bfloat16).astype(jnp.float32)
+        both = jnp.concatenate([high, tile - high], axis=0)
+        lam_pair[slot // 2, :, cols] = jnp.where(row_no % 8 == 0, both, 0.0).astype(jnp.bfloat16)
+
+    for b in range(S):
+        put_lambda(b, lam_exp[m * S + b, d])
+    for t in range(T):
+        tile = jnp.zeros((8, C), jnp.float32)
+        for way in range(2):
+            q = lax.rem((r - (t // P + 1) if way == 0 else r + (t // P + 1)) + 2 * N, N)
+            q_m = jnp.where(q < D, 0, 1)
+            q_d = jnp.where(q < D, q, N - 1 - q)
+            p = t % P if way == 0 else P - 1 - t % P
+            for b in range(S):
+                place = b * 2 + way
+                values = lam_exp[q_m * S + b, q_d]
+                if place != p:
+                    values = pltpu.roll(values, ((place - p) * PR) % C, 1)
+                tile = jnp.where(lane_no == place, values, tile)
+        put_lambda(S + t, tile)
+
+    first = pl.multiple_of(me * rows, LANES)
+    chunk = min(H, 256)
+
+    def gradient(u, begin):
+        at = (xs[u, :, pl.ds(first, rows)].astype(jnp.float32).T * lam_row[u, 0:1, :]).astype(
+            jnp.bfloat16
+        )
+        pair = lam_pair[u]
+        for c in range(0, H, chunk):
+            cols = slice(c, c + chunk)
+            grad = jnp.dot(at, slope[u, :, cols], preferred_element_type=jnp.float32)
+            top = jnp.dot(pair, hid[u, :, cols], preferred_element_type=jnp.float32)
+            if begin:
+                w1g_ref[:, cols] = grad
+                wtot[:, cols] = top
+            else:
+                w1g_ref[:, cols] += grad
+                wtot[:, cols] += top
+
+    gradient(0, True)
+    relay(late)
+    step_forward(late - 1)
+    gradient(1, False)
+    done = (S + T) // 2 - 1
+    behind = late + 1 - (done - (T - 2 - late))
+    for u in range(2, late + 1 - behind):
+        gradient(u, False)
+
+    def full_step(t, carry):
+        relay(t)
+        step_forward(t - 1)
+        gradient(t - behind, False)
+        return carry
+
+    lax.fori_loop(late + 1, T - 1, full_step, 0)
+    relay(T - 1)
+    step_forward(T - 2)
+    step_forward(T - 1)
+    gradient(done, False)
+    w1g_ref[...] = w1g_ref[...] * w2
+    w2g_ref[...] = jnp.sum(wtot[...], axis=0, keepdims=True)
+
+    own_twin.wait_send()
+    for k in range(1, D):
+        info_copy(k).wait_send()
+    for a, b in lane_steps:
+        lam_copy(a, b).wait_send()
+
+    def drain(t, carry):
+        ahead_copy(part(S + t, s, 0), t).wait_send()
+        behind_copy(part(S + t, s, 1), t).wait_send()
+        twin_copy(S + t, s).wait_send()
+        return carry
+
+    lax.fori_loop(0, T, drain, 0)
+
+
+def ring_call(sizes, operands):
+    D, M, S, C, E, H, rows, P = sizes
+    L, N = M * S, D * M
+    T = P * (N - 1) // 2
+    f32, bf16 = jnp.float32, jnp.bfloat16
+    vmem = pl.BlockSpec(memory_space=pltpu.VMEM)
+    hbm = pl.BlockSpec(memory_space=pl.ANY)
+    dma = pltpu.SemaphoreType.DMA
+    slots = S + T
+    crossing = max(min(2 * (D - 1 - i), 2 * i) + 1 for i in range(D))
+    stages = max(D - 1, crossing + 1) - 1
+    scratch = [
+        pltpu.VMEM((E, H), bf16),
+        pltpu.VMEM((slots // 2, 2 * C, E), bf16),
+        pltpu.VMEM((slots // 2, 2 * C, H), bf16),
+        pltpu.VMEM((slots // 2, 2 * C, H), bf16),
+        pltpu.VMEM((3, 1, C), jnp.int32),
+        pltpu.VMEM((1, H), f32),
+        pltpu.VMEM((C, E), f32),
+        pltpu.VMEM((16, H), f32),
+        pltpu.VMEM((D, 8, C), f32),
+        pltpu.VMEM((D, 8, C), f32),
+        pltpu.VMEM((D, 8, C), f32),
+        pltpu.VMEM((L, 8, C), f32),
+        pltpu.VMEM((L, D, 8, C), f32),
+        pltpu.VMEM((slots // 2, 8, 2 * C), f32),
+        pltpu.VMEM((slots // 2, 16, 2 * C), bf16),
+        dma((6,)),
+        dma((T,)), dma((T,)), dma((T,)), dma((T,)),
+        dma((slots,)), dma((slots,)),
+        dma((D,)), dma((D,)),
+        dma((L,)), dma((L,)),
+        pltpu.SemaphoreType.REGULAR((stages,)),
+    ]
+    return pl.pallas_call(
+        functools.partial(ring_kernel, sizes),
+        out_shape=(
+            pltpu.VMEM((C, E), bf16),
+            pltpu.VMEM((rows, H), f32),
+            pltpu.VMEM((1, H), f32),
+        ),
+        in_specs=[hbm] * 6,
+        out_specs=(vmem, vmem, vmem),
+        scratch_shapes=scratch,
+        compiler_params=pltpu.CompilerParams(
+            collective_id=0, has_side_effects=True, vmem_limit_bytes=56 * 1024 * 1024
+        ),
+    )(*operands)
+
 
 def write_out(a_ref, b_ref, c_ref, a_out, b_out, c_out, sem):
     pairs = ((b_ref, b_out), (a_ref, a_out), (c_ref, c_out))
@@ -340,12 +718,9 @@
         copy.wait()
 
 
-def on_device(embeddings, owner_shard, query_local, labels, w_first, w_second):
-    D, M, S = lax.axis_size("docs"), lax.axis_size("mp"), lax.axis_size("sub")
-    C, E = embeddings.shape
-    H = w_first.shape[1]
+def reduce_call(sizes, operands):
+    D, M, S, C, E, H, rows = sizes
     L = M * S
-    rows = E // L
     width = max(rows, LANES)
     Kc = 4
     Kr = max(1, rows // 32)
@@ -381,7 +756,7 @@
         dma((D,)), dma((D,)),
         dma((K,)), dma((K,)), dma((K,)), dma((K,)),
     ]
-    emb_grad, w1g, w2g = pl.pallas_call(
+    return pl.pallas_call(
         functools.partial(kernel, (D, M, S, C, E, H, rows, Kc, Kr)),
         out_shape=(
             pltpu.VMEM((C, E), bf16),
@@ -394,10 +769,32 @@
         compiler_params=pltpu.CompilerParams(
             collective_id=0, has_side_effects=True, vmem_limit_bytes=56 * 1024 * 1024
         ),
-    )(
+    )(*operands)
+
+
+def on_device(embeddings, owner_shard, query_local, labels, w_first, w_second):
+    D, M, S = lax.axis_size("docs"), lax.axis_size("mp"), lax.axis_size("sub")
+    C, E = embeddings.shape
+    H = w_first.shape[1]
+    L = M * S
+    rows = E // L
+    vmem = pl.BlockSpec(memory_space=pltpu.VMEM)
+    hbm = pl.BlockSpec(memory_space=pl.ANY)
+    dma = pltpu.SemaphoreType.DMA
+    operands = (
         embeddings, w_first, owner_shard.reshape(1, C), query_local.reshape(1, C),
         labels.reshape(1, C), w_second.reshape(1, H),
     )
+    P = 2 * S
+    held = D * L * C * (E + 2 * H) * 2
+    gathers = (
+        M == 2 and S == 2 and D > 1 and C == LANES and rows % LANES == 0 and held <= 32 * 2**20
+    )
+    if gathers:
+        outs = ring_call((D, M, S, C, E, H, rows, P), operands)
+    else:
+        outs = reduce_call((D, M, S, C, E, H, rows), operands)
+    emb_grad, w1g, w2g = outs
     emb_grad, w1g, w2g = pl.pallas_call(
         write_out,
         out_shape=tuple(jax.ShapeDtypeStruct(v.shape, v.dtype) for v in (emb_grad, w1g, w2g)),

time: 38.1 us -> 30.2 us (0.79)
  Pallas kernels: 37.2 us -> 29.5 us
    pallas_call x1, Pallas kernels: 36.1 us -> 28.4 us  [ring_call(): pl.pallas_call(functools.partial(ring_kernel, sizes), out_shape=(pltpu.VM...]
where the time goes in v2:
time: 30.2 us; the launch traced here: 30.1 us
  Pallas kernels  29.5 us (98%)
  between operations  0.64 us (2%)
    pallas_call x1, Pallas kernels, ring_call(): pl.pallas_call(functools.partial(ring_kernel, sizes), out_shape=(pltpu.VM...  28.4 us
    pallas_call x1, Pallas kernels, on_device(): pl.pallas_call(write_out, out_shape=tuple((jax.ShapeDtypeStruct(v.shape,...  1.08 us

profile of v2, /device:TPU:0, one launch (start us, length us, event | category | flops | bytes accessed | tf_op | source)
XLA Modules:
  0.0 30.1 jit_solution(16883230632689756983)
XLA Ops:
  0.6 28.4 %shard_map.85 = (bf16[128,1024]{1,0:T(8,128)(2,1)S(1)}, f32[256,1024]{1,0:T(8,128)S(1)}, f32[1,1024]{1,0:T(1,128)S(1)}) custom-call(bf16[128,1024]{1,0:T(8,128)(2,1)} %emb_hbm.1, bf16[1024,1024]{1,0:T(8,128)(2,1)} %w1_hbm.1, s32[1,128]{1,0:T(1,128)} %bitcast.6, s32[1,128]{1,0:T(1,128)} %bitcast.7, s32[1,128]{1,0:T(1,128)} %bitcast.8, f32[1,1024]{1,0:T(1,128)} %bitcast.5), custom_call_target="tpu_custom_call" | custom-call | tf_op jit(solution)/shard_map/pallas_call | solution.py:696
  29.0 1.1 %shard_map.86 = (bf16[128,1024]{1,0:T(8,128)(2,1)}, f32[256,1024]{1,0:T(8,128)}, f32[1,1024]{1,0:T(1,128)}) custom-call(bf16[128,1024]{1,0:T(8,128)(2,1)S(1)} %get-tuple-element.9.a_ref, f32[256,1024]{1,0:T(8,128)S(1)} %get-tuple-element.10.b_ref, f32[1,1024]{1,0:T(1,128)S(1)} %get-tuple-element.11.c_ref), custom_call_target="tpu_custom_call" | custom-call | tf_op jit(solution)/shard_map/pallas_call | solution.py:798

commit v3 on v2

--- a/solution.py
+++ b/solution.py
@@ -333,11 +333,10 @@
 def ring_kernel(
     sizes,
     emb_hbm, w1_hbm, owner_hbm, local_hbm, labels_hbm, w2_hbm,
-    emb_grad_ref, w1g_ref, w2g_ref,
-    w1v, xs, slope, hid, small, w2v, pre, wtot,
+    emb_grad_ref, w1g_ref, wtot, at_end, pair_end, slope_end, hid_end, w2v,
+    w1v, xs, slope, hid, small, pre,
     info, term, drow, lam_all, lam_exp, lam_row, lam_pair,
-    load_sem, cw_send, cw_recv, ccw_send, ccw_recv, dd_send, dd_recv,
-    i_send, i_recv, l_send, l_recv, stage_sem,
+    load_sem, ring_recv, twin_recv, own_sem, info_sem, lam_sem, send_sem, stage_sem,
 ):
     D, M, S, C, E, H, rows, P = sizes
     N = D * M
@@ -387,16 +386,23 @@
         return block(slot).at[pl.ds((lane_s * 2 + way) * PR, PR)]
 
     def ahead_copy(src, t):
-        return remote(src, part(S + t, s, 0), cw_send.at[t], cw_recv.at[t], ahead_id)
+        return remote(src, part(S + t, s, 0), send_sem.at[0], ring_recv.at[t], ahead_id)
 
     def behind_copy(src, t):
-        return remote(src, part(S + t, s, 1), ccw_send.at[t], ccw_recv.at[t], behind_id)
-
-    def twin_copy(slot, lane_s):
-        both = block(slot).at[pl.ds(lane_s * 2 * PR, 2 * PR)]
-        return remote(both, both, dd_send.at[slot], dd_recv.at[slot], twin_id)
-
-    own_twin = remote(block(s), block(s), dd_send.at[0], dd_recv.at[0], twin_id)
+        return remote(src, part(S + t, s, 1), send_sem.at[0], ring_recv.at[t], behind_id)
+
+    def both_ways(slot, lane_s):
+        return block(slot).at[pl.ds(lane_s * 2 * PR, 2 * PR)]
+
+    def ring_wait(t):
+        both = both_ways(S + t, s)
+        remote(both, both, send_sem.at[0], ring_recv.at[t], ahead_id).wait_recv()
+
+    def twin_copy(t, lane_s):
+        both = both_ways(S + t, lane_s)
+        return remote(both, both, send_sem.at[0], twin_recv.at[t], twin_id)
+
+    own_twin = remote(block(s), block(s), own_sem.at[0], own_sem.at[1], twin_id)
 
     def next_stage(k):
         for peer in (ahead_id, behind_id):
@@ -411,7 +417,7 @@
         ahead_copy(block(s).at[pl.ds(p * PR, PR)], p).start()
         behind_copy(block(s).at[pl.ds((P - 1 - p) * PR, PR)], p).start()
 
-    for p in range(P // 2):
+    for p in range(P - 1):
         send_own(p)
     own_twin.start()
     stages = stage_sem.shape[0]
@@ -421,6 +427,8 @@
         copy.wait()
     load_w.wait()
     w2 = w2v[...]
+
+    ends = (S + T) // 2 - 1
 
     def forward(slot):
         u, row = spot(slot)
@@ -428,8 +436,12 @@
         sg = 0.5 + 0.5 * jnp.tanh(0.5 * act)
         hidden = act * sg
         bend = sg + hidden * (1.0 - sg)
-        hid[u, pl.ds(row, C), :] = hidden.astype(jnp.bfloat16)
-        slope[u, pl.ds(row, C), :] = bend.astype(jnp.bfloat16)
+        if isinstance(slot, int) and slot // 2 == ends:
+            hid_end[pl.ds(slot % 2 * C, C), :] = hidden.astype(jnp.bfloat16)
+            slope_end[pl.ds(slot % 2 * C, C), :] = bend.astype(jnp.bfloat16)
+        else:
+            hid[u, pl.ds(row, C), :] = hidden.astype(jnp.bfloat16)
+            slope[u, pl.ds(row, C), :] = bend.astype(jnp.bfloat16)
         return hidden, bend
 
     hidden, bend = forward(s)
@@ -448,16 +460,18 @@
 
     def info_copy(k):
         return remote(
-            info.at[d], info.at[d], i_send.at[k], i_recv.at[k], {"docs": doc_peer(k)}
+            info.at[d], info.at[d], info_sem.at[0], info_sem.at[1], {"docs": doc_peer(k)}
         )
 
     lane_steps = [(a, b) for a in range(M) for b in range(S) if a or b]
 
     def lam_copy(a, b):
         peer = {"mp": lax.rem(m + a, M), "sub": lax.rem(s + b, S)}
-        return remote(
-            lam_all.at[me], lam_all.at[me], l_send.at[a * S + b], l_recv.at[a * S + b], peer
-        )
+        return remote(lam_all.at[me], lam_all.at[me], lam_sem.at[0], lam_sem.at[1], peer)
+
+    infos, lams = info.at[pl.ds(0, D - 1)], lam_all.at[pl.ds(0, M * S - 1)]
+    info_both = remote(infos, infos, info_sem.at[0], info_sem.at[1], twin_id)
+    lam_both = remote(lams, lams, lam_sem.at[0], lam_sem.at[1], twin_id)
 
     reach = min(stages, max(1, D - 2))
     for k in range(2, reach + 1):
@@ -466,28 +480,22 @@
             next_stage(k)
     for k in range(1, D):
         info_copy(k).start()
-    for p in range(P // 2, P):
-        send_own(p)
+    send_own(P - 1)
     own_twin.wait_recv()
     forward(other)
 
     def relay(t):
-        ahead_copy(part(S + t, s, 0), t).wait_recv()
+        ring_wait(t)
 
         @pl.when(t + P < T)
         def _():
             ahead_copy(part(S + t, s, 0), t + P).start()
-
-        behind_copy(part(S + t, s, 1), t).wait_recv()
-
-        @pl.when(t + P < T)
-        def _():
             behind_copy(part(S + t, s, 1), t + P).start()
 
-        twin_copy(S + t, s).start()
+        twin_copy(t, s).start()
 
     def step_forward(t):
-        twin_copy(S + t, other).wait_recv()
+        twin_copy(t, other).wait_recv()
         forward(S + t)
 
     def relay_forward(lag, t, carry):
@@ -499,8 +507,7 @@
     relay(0)
     lax.fori_loop(1, early, functools.partial(relay_forward, 1), 0)
 
-    for k in range(1, D):
-        info_copy(k).wait_recv()
+    info_both.wait_recv()
     slot_of = lax.broadcasted_iota(jnp.int32, (1, C), 1).astype(jnp.float32)
     total = float(D * C)
 
@@ -569,8 +576,8 @@
     lax.fori_loop(early + 1, late, functools.partial(relay_forward, 2), 0)
     step_forward(late - 2)
 
+    lam_both.wait_recv()
     for a, b in lane_steps:
-        lam_copy(a, b).wait_recv()
         lane = lax.rem(m + M - a, M) * S + lax.rem(s + S - b, S)
         for i in range(D):
             lam_exp[lane, i] = jnp.broadcast_to(lam_all[lane, i : i + 1, :], (8, C))
@@ -605,10 +612,13 @@
     first = pl.multiple_of(me * rows, LANES)
     chunk = min(H, 256)
 
+    def turned(u):
+        return (xs[u, :, pl.ds(first, rows)].astype(jnp.float32).T * lam_row[u, 0:1, :]).astype(
+            jnp.bfloat16
+        )
+
     def gradient(u, begin):
-        at = (xs[u, :, pl.ds(first, rows)].astype(jnp.float32).T * lam_row[u, 0:1, :]).astype(
-            jnp.bfloat16
-        )
+        at = turned(u)
         pair = lam_pair[u]
         for c in range(0, H, chunk):
             cols = slice(c, c + chunk)
@@ -625,8 +635,7 @@
     relay(late)
     step_forward(late - 1)
     gradient(1, False)
-    done = (S + T) // 2 - 1
-    behind = late + 1 - (done - (T - 2 - late))
+    behind = late + 1 - (ends - (T - 2 - late))
     for u in range(2, late + 1 - behind):
         gradient(u, False)
 
@@ -636,27 +645,20 @@
         gradient(t - behind, False)
         return carry
 
-    lax.fori_loop(late + 1, T - 1, full_step, 0)
+    lax.fori_loop(late + 1, T - 2, full_step, 0)
+    relay(T - 2)
+    step_forward(T - 3)
     relay(T - 1)
+    gradient(T - 2 - behind, False)
     step_forward(T - 2)
+    pair_end[...] = lam_pair[ends]
+    own_twin.wait_send()
+    info_both.wait_send()
+    lam_both.wait_send()
     step_forward(T - 1)
-    gradient(done, False)
-    w1g_ref[...] = w1g_ref[...] * w2
-    w2g_ref[...] = jnp.sum(wtot[...], axis=0, keepdims=True)
-
-    own_twin.wait_send()
-    for k in range(1, D):
-        info_copy(k).wait_send()
-    for a, b in lane_steps:
-        lam_copy(a, b).wait_send()
-
-    def drain(t, carry):
-        ahead_copy(part(S + t, s, 0), t).wait_send()
-        behind_copy(part(S + t, s, 1), t).wait_send()
-        twin_copy(S + t, s).wait_send()
-        return carry
-
-    lax.fori_loop(0, T, drain, 0)
+    at_end[...] = turned(ends)
+    sent = xs.at[pl.ds(0, T // 2)]
+    remote(sent, sent, send_sem.at[0], ring_recv.at[0], twin_id).wait_send()
 
 
 def ring_call(sizes, operands):
@@ -676,9 +678,7 @@
         pltpu.VMEM((slots // 2, 2 * C, H), bf16),
         pltpu.VMEM((slots // 2, 2 * C, H), bf16),
         pltpu.VMEM((3, 1, C), jnp.int32),
-        pltpu.VMEM((1, H), f32),
         pltpu.VMEM((C, E), f32),
-        pltpu.VMEM((16, H), f32),
         pltpu.VMEM((D, 8, C), f32),
         pltpu.VMEM((D, 8, C), f32),
         pltpu.VMEM((D, 8, C), f32),
@@ -686,27 +686,65 @@
         pltpu.VMEM((L, D, 8, C), f32),
         pltpu.VMEM((slots // 2, 8, 2 * C), f32),
         pltpu.VMEM((slots // 2, 16, 2 * C), bf16),
-        dma((6,)),
-        dma((T,)), dma((T,)), dma((T,)), dma((T,)),
-        dma((slots,)), dma((slots,)),
-        dma((D,)), dma((D,)),
-        dma((L,)), dma((L,)),
+        dma((6,)), dma((T,)), dma((T,)), dma((2,)), dma((2,)), dma((2,)), dma((1,)),
         pltpu.SemaphoreType.REGULAR((stages,)),
     ]
-    return pl.pallas_call(
+    held = pl.pallas_call(
         functools.partial(ring_kernel, sizes),
         out_shape=(
             pltpu.VMEM((C, E), bf16),
             pltpu.VMEM((rows, H), f32),
+            pltpu.VMEM((16, H), f32),
+            pltpu.VMEM((rows, 2 * C), bf16),
+            pltpu.VMEM((16, 2 * C), bf16),
+            pltpu.VMEM((2 * C, H), bf16),
+            pltpu.VMEM((2 * C, H), bf16),
             pltpu.VMEM((1, H), f32),
         ),
         in_specs=[hbm] * 6,
-        out_specs=(vmem, vmem, vmem),
+        out_specs=(vmem,) * 8,
         scratch_shapes=scratch,
         compiler_params=pltpu.CompilerParams(
             collective_id=0, has_side_effects=True, vmem_limit_bytes=56 * 1024 * 1024
         ),
     )(*operands)
+    return pl.pallas_call(
+        finish,
+        out_shape=(
+            jax.ShapeDtypeStruct((C, E), bf16),
+            jax.ShapeDtypeStruct((rows, H), f32),
+            jax.ShapeDtypeStruct((1, H), f32),
+        ),
+        in_specs=[vmem] * 8,
+        out_specs=(hbm,) * 3,
+        scratch_shapes=[pltpu.VMEM((rows, H), f32), pltpu.VMEM((1, H), f32), dma((6,))],
+        compiler_params=pltpu.CompilerParams(vmem_limit_bytes=4 * 1024 * 1024),
+    )(*held)
+
+
+def finish(
+    emb_grad, w1g, wtot, at, pair, slope, hid, w2, emb_out, w1g_out, w2g_out, w1g_end, w2g_end, sem
+):
+    H = w2.shape[1]
+    parts = 4
+    wide = H // parts
+    copies = [pltpu.make_async_copy(emb_grad, emb_out, sem.at[0])]
+    copies[0].start()
+    for c in range(parts):
+        cols = slice(c * wide, (c + 1) * wide)
+        if c == parts - 1:
+            top = wtot[...] + jnp.dot(pair[...], hid[...], preferred_element_type=jnp.float32)
+            w2g_end[...] = jnp.sum(top, axis=0, keepdims=True)
+            copies.append(pltpu.make_async_copy(w2g_end, w2g_out, sem.at[1]))
+            copies[-1].start()
+        grad = jnp.dot(at[...], slope[:, cols], preferred_element_type=jnp.float32)
+        w1g_end[:, cols] = (w1g[:, cols] + grad) * w2[:, cols]
+        copies.append(
+            pltpu.make_async_copy(w1g_end.at[:, cols], w1g_out.at[:, cols], sem.at[2 + c])
+        )
+        copies[-1].start()
+    for copy in copies:
+        copy.wait()
 
 
 def write_out(a_ref, b_ref, c_ref, a_out, b_out, c_out, sem):
@@ -791,10 +829,9 @@
         M == 2 and S == 2 and D > 1 and C == LANES and rows % LANES == 0 and held <= 32 * 2**20
     )
     if gathers:
-        outs = ring_call((D, M, S, C, E, H, rows, P), operands)
-    else:
-        outs = reduce_call((D, M, S, C, E, H, rows), operands)
-    emb_grad, w1g, w2g = outs
+        emb_grad, w1g, w2g = ring_call((D, M, S, C, E, H, rows, P), operands)
+        return emb_grad, w1g, w2g.reshape(H)
+    emb_grad, w1g, w2g = reduce_call((D, M, S, C, E, H, rows), operands)
     emb_grad, w1g, w2g = pl.pallas_call(
         write_out,
         out_shape=tuple(jax.ShapeDtypeStruct(v.shape, v.dtype) for v in (emb_grad, w1g, w2g)),

time: 30.2 us -> 28.9 us (0.957)
  Pallas kernels: 29.5 us -> 28.1 us
    pallas_call x1, Pallas kernels: 28.4 us -> 26.9 us  [ring_call(): pl.pallas_call(functools.partial(ring_kernel, sizes), out_shape=(pltpu.VM...]
where the time goes in v3:
time: 28.9 us; the launch traced here: 28.8 us
  Pallas kernels  28.1 us (97%)
  between operations  0.64 us (2%)
    pallas_call x1, Pallas kernels, ring_call(): pl.pallas_call(functools.partial(ring_kernel, sizes), out_shape=(pltpu.VM...  26.9 us
    pallas_call x1, Pallas kernels, ring_call(): pl.pallas_call(finish, out_shape=(jax.ShapeDtypeStruct((C, E), bf16), jax...  1.24 us

profile of v3, /device:TPU:0, one launch (start us, length us, event | category | flops | bytes accessed | tf_op | source)
XLA Modules:
  0.0 28.8 jit_solution(14380413159236045274)
XLA Ops:
  0.6 26.9 %shard_map.85 = (bf16[128,1024]{1,0:T(8,128)(2,1)S(1)}, f32[256,1024]{1,0:T(8,128)S(1)}, f32[16,1024]{1,0:T(8,128)S(1)}, bf16[256,256]{1,0:T(8,128)(2,1)S(1)}, b...) custom-call(bf16[128,1024]{1,0:T(8,128)(2,1)} %emb_hbm.1, ...), custom_call_target="tpu_custom_call" | custom-call | tf_op jit(solution)/shard_map/pallas_call | solution.py:692
  27.5 1.2 %shard_map.86 = (bf16[128,1024]{1,0:T(8,128)(2,1)}, f32[256,1024]{1,0:T(8,128)}, f32[1,1024]{1,0:T(1,128)}) custom-call(bf16[128,1024]{1,0:T(8,128)(2,1)S(1)} %get-tuple-element.14.emb_grad, f32[256,1024]{1,0:T(8,128)S(1)} %get-tuple-element.15.w1g, f32[16,1024]{1,0:T(8,128)S(1)} %get-tuple-element.16.wtot, bf16[256,256]{1,0:T(8,128)(2,1)S(1)} %get-tuple-element.17.at, ...), custom_call_target="tpu_custom_call" | custom-call | tf_op jit(solution)/shard_map/pallas_call | solution.py:711

commit v4 on v3

--- a/solution.py
+++ b/solution.py
@@ -330,13 +330,17 @@
     for k in range(K):
         pl.when(has_out)(lambda k=k: send_out(k, False).wait_send())
 
+LEAD = 2
+PARTS = 4
+
+
 def ring_kernel(
     sizes,
     emb_hbm, w1_hbm, owner_hbm, local_hbm, labels_hbm, w2_hbm,
-    emb_grad_ref, w1g_ref, wtot, at_end, pair_end, slope_end, hid_end, w2v,
-    w1v, xs, slope, hid, small, pre,
+    emb_grad_ref, w1g_ref, w2g_ref, at_end, slope_end, w2v,
+    w1v, xs, slope, hid, small, pre, wtot,
     info, term, drow, lam_all, lam_exp, lam_row, lam_pair,
-    load_sem, ring_recv, twin_recv, own_sem, info_sem, lam_sem, send_sem, stage_sem,
+    load_sem, ring_recv, twin_recv, own_sem, info_sem, lam_sem, send_sem, stage_sem, up_sem,
 ):
     D, M, S, C, E, H, rows, P = sizes
     N = D * M
@@ -369,8 +373,25 @@
         pltpu.make_async_copy(w2_hbm, w2v, load_sem.at[5]),
     ]
     barrier = pltpu.get_barrier_semaphore()
-    for peer in (ahead_id, behind_id, twin_id):
+
+    def flows(act):
+        def of(first, second):
+            pl.when(m == 0)(lambda: act(*first))
+            pl.when(m > 0)(lambda: act(*second))
+
+        return of
+
+    @flows
+    def hello_up(peer):
         pl.semaphore_signal(barrier, inc=1, device_id=peer, device_id_type=MESH)
+
+    pl.semaphore_signal(barrier, inc=1, device_id=twin_id, device_id_type=MESH)
+    hello_up((ahead_id,), (behind_id,))
+
+    @pl.when((d == 0) | (d == D - 1))
+    def _():
+        hello_up((behind_id,), (ahead_id,))
+
     load_e.start()
     load_w.start()
     for copy in load_small:
@@ -411,15 +432,40 @@
     def stage_wait(k):
         pl.semaphore_wait(stage_sem.at[k], 2)
 
-    pl.semaphore_wait(barrier, 3)
+    def send_ahead(p):
+        ahead_copy(block(s).at[pl.ds(p * PR, PR)], p).start()
+
+    def send_behind(p):
+        behind_copy(block(s).at[pl.ds((P - 1 - p) * PR, PR)], p).start()
+
+    def send_both(p):
+        send_ahead(p)
+        send_behind(p)
+
+    @flows
+    def send_first(send):
+        for p in range(P - 1):
+            send(p)
+
+    @flows
+    def answer(peer):
+        pl.semaphore_signal(up_sem.at[0], inc=1, device_id=peer, device_id_type=MESH)
+
+    pl.semaphore_wait(barrier, jnp.where(d >= D - 2, 3, 2))
+
+    @pl.when((d > 0) & (d < D - 1))
+    def _():
+        answer((behind_id,), (ahead_id,))
+
     load_e.wait()
-    def send_own(p):
-        ahead_copy(block(s).at[pl.ds(p * PR, PR)], p).start()
-        behind_copy(block(s).at[pl.ds((P - 1 - p) * PR, PR)], p).start()
-
-    for p in range(P - 1):
-        send_own(p)
+    send_first((send_behind,), (send_ahead,))
     own_twin.start()
+
+    @pl.when(d < D - 2)
+    def _():
+        pl.semaphore_wait(up_sem.at[0], 1)
+
+    send_first((send_ahead,), (send_behind,))
     stages = stage_sem.shape[0]
     next_stage(0)
 
@@ -429,6 +475,9 @@
     w2 = w2v[...]
 
     ends = (S + T) // 2 - 1
+
+    early, late = T // 4 + 1, T // 2 + 2
+    direct = (S + late + 1) // 2
 
     def forward(slot):
         u, row = spot(slot)
@@ -436,18 +485,22 @@
         sg = 0.5 + 0.5 * jnp.tanh(0.5 * act)
         hidden = act * sg
         bend = sg + hidden * (1.0 - sg)
-        if isinstance(slot, int) and slot // 2 == ends:
-            hid_end[pl.ds(slot % 2 * C, C), :] = hidden.astype(jnp.bfloat16)
+        known = isinstance(slot, int)
+        if known and slot // 2 == ends:
             slope_end[pl.ds(slot % 2 * C, C), :] = bend.astype(jnp.bfloat16)
         else:
+            slope[u, pl.ds(row, C), :] = bend.astype(jnp.bfloat16)
+        if known and slot // 2 >= direct:
+            column = across(lam_row[slot // 2, 0:1, slot % 2 * C : slot % 2 * C + C], C)[:, 0:1]
+            w2g_ref[...] += jnp.sum(hidden * column, axis=0, keepdims=True)
+        else:
             hid[u, pl.ds(row, C), :] = hidden.astype(jnp.bfloat16)
-            slope[u, pl.ds(row, C), :] = bend.astype(jnp.bfloat16)
         return hidden, bend
 
     hidden, bend = forward(s)
-    info[d] = row_tile(jnp.sum(hidden * w2, axis=1, keepdims=True))
-    info[d, 1:2, :] = small[2].astype(jnp.float32)
-    info[d, 2:3, :] = (small[0] * 1024 + small[1]).astype(jnp.float32)
+    info[d, 0] = row_tile(jnp.sum(hidden * w2, axis=1, keepdims=True))[0:1, :]
+    info[d, 1] = small[2].astype(jnp.float32)
+    info[d, 2] = (small[0] * 1024 + small[1]).astype(jnp.float32)
     stage_wait(0)
     if stages > 1:
         next_stage(1)
@@ -480,7 +533,7 @@
             next_stage(k)
     for k in range(1, D):
         info_copy(k).start()
-    send_own(P - 1)
+    send_both(P - 1)
     own_twin.wait_recv()
     forward(other)
 
@@ -494,34 +547,44 @@
 
         twin_copy(t, s).start()
 
+    def lead_relay(t):
+        q = t + LEAD * s
+        if isinstance(t, int) and t + LEAD * (S - 1) < T:
+            relay(q)
+        else:
+            pl.when(q < T)(lambda: relay(q))
+
     def step_forward(t):
         twin_copy(t, other).wait_recv()
         forward(S + t)
 
-    def relay_forward(lag, t, carry):
-        relay(t)
-        step_forward(t - lag)
+    def relay_forward(t, carry):
+        lead_relay(t)
+        step_forward(t)
         return carry
 
-    early, late = T // 4 + 1, T // 2 + 1
-    relay(0)
-    lax.fori_loop(1, early, functools.partial(relay_forward, 1), 0)
+    @pl.when(s > 0)
+    def _():
+        for t in range(LEAD):
+            relay(t)
+
+    lax.fori_loop(0, early, relay_forward, 0)
 
     info_both.wait_recv()
     slot_of = lax.broadcasted_iota(jnp.int32, (1, C), 1).astype(jnp.float32)
     total = float(D * C)
 
     def key_of(jd):
-        return info[jd, 1:2, :] * total - (slot_of + lax.convert_element_type(jd * C, jnp.float32))
+        return info[jd, 1] * total - (slot_of + lax.convert_element_type(jd * C, jnp.float32))
 
     def rank_step(jd, carry):
-        q_j = across(info[jd, 2:3, :], C)
-        s_j = across(info[jd, 0:1, :], C)
+        q_j = across(info[jd, 2], C)
+        s_j = across(info[jd, 0], C)
         key_j = across(key_of(jd), C)
         out = []
         for i in range(D):
-            same = q_j == info[i, 2:3, :]
-            push = 0.5 + 0.5 * jnp.tanh(0.5 * (s_j - info[i, 0:1, :]))
+            same = q_j == info[i, 2]
+            push = 0.5 + 0.5 * jnp.tanh(0.5 * (s_j - info[i, 0]))
             ahead = same & (key_j > key_of(i))
             out.append(carry[i] + jnp.sum(jnp.where(same, push, 0.0), axis=0, keepdims=True))
             out.append(carry[D + i] + jnp.sum(jnp.where(ahead, 1.0, 0.0), axis=0, keepdims=True))
@@ -530,23 +593,23 @@
     zeros = tuple(jnp.zeros((1, C), jnp.float32) for _ in range(2 * D))
     ranks = lax.fori_loop(0, D, rank_step, zeros)
     for i in range(D):
-        gain = jnp.exp2(info[i, 1:2, :]) - 1.0
+        gain = jnp.exp2(info[i, 1]) - 1.0
         term[i, 0:1, :] = gain / log2(2.0 + ranks[D + i])
         drow[i, 0:1, :] = 1.0 / log2(2.0 + (ranks[i] - 0.5))
 
-    relay(early)
+    pl.when(s == 0)(lambda: relay(early))
 
     def lambda_step(jd, carry):
-        q_j = across(info[jd, 2:3, :], C)
-        s_j = across(info[jd, 0:1, :], C)
-        gain_j = across(jnp.exp2(info[jd, 1:2, :]) - 1.0, C)
+        q_j = across(info[jd, 2], C)
+        s_j = across(info[jd, 0], C)
+        gain_j = across(jnp.exp2(info[jd, 1]) - 1.0, C)
         disc_j = across(drow[jd, 0:1, :], C)
         term_j = across(term[jd, 0:1, :], C)
         out = []
         for i in range(D):
-            same = q_j == info[i, 2:3, :]
-            gain_i = jnp.exp2(info[i, 1:2, :]) - 1.0
-            gap = info[i, 0:1, :] - s_j
+            same = q_j == info[i, 2]
+            gain_i = jnp.exp2(info[i, 1]) - 1.0
+            gap = info[i, 0] - s_j
             weight = (gain_j - gain_i) * jnp.abs(drow[i, 0:1, :] - disc_j)
             push = 0.5 + 0.5 * jnp.tanh(0.5 * jnp.where(gain_i > gain_j, -gap, gap))
             out.append(
@@ -561,7 +624,7 @@
     for i in range(D):
         idcg = sums[D + i]
         inv = jnp.where(idcg > 0.0, 1.0 / jnp.where(idcg > 0.0, idcg, 1.0), 0.0)
-        lam_all[me, i : i + 1, :] = sums[i] * inv
+        lam_all[me, i] = sums[i] * inv
     for k in range(reach + 1, stages + 1):
         stage_wait(k - 1)
         if k < stages:
@@ -570,17 +633,20 @@
         lam_copy(a, b).start()
 
     for i in range(D):
-        lam_exp[me, i] = jnp.broadcast_to(lam_all[me, i : i + 1, :], (8, C))
+        lam_exp[me, i] = jnp.broadcast_to(lam_all[me, i], (8, C))
     emb_grad_ref[...] = (pre[...] * across(lam_exp[me, d, 0:1, :], C)[:, 0:1]).astype(jnp.bfloat16)
 
-    lax.fori_loop(early + 1, late, functools.partial(relay_forward, 2), 0)
-    step_forward(late - 2)
+    pl.when(s > 0)(lambda: relay(early + LEAD))
+    lead_relay(early + 1)
+    step_forward(early)
+    step_forward(early + 1)
+    lax.fori_loop(early + 2, late, relay_forward, 0)
 
     lam_both.wait_recv()
     for a, b in lane_steps:
         lane = lax.rem(m + M - a, M) * S + lax.rem(s + S - b, S)
         for i in range(D):
-            lam_exp[lane, i] = jnp.broadcast_to(lam_all[lane, i : i + 1, :], (8, C))
+            lam_exp[lane, i] = jnp.broadcast_to(lam_all[lane, i], (8, C))
 
     lane_no = lax.broadcasted_iota(jnp.int32, (8, C), 1) // PR
     row_no = lax.broadcasted_iota(jnp.int32, (16, C), 0)
@@ -612,51 +678,43 @@
     first = pl.multiple_of(me * rows, LANES)
     chunk = min(H, 256)
 
-    def turned(u):
-        return (xs[u, :, pl.ds(first, rows)].astype(jnp.float32).T * lam_row[u, 0:1, :]).astype(
-            jnp.bfloat16
-        )
+    def turned(u, begin=0, count=2 * C):
+        values = xs[u, begin : begin + count, pl.ds(first, rows)].astype(jnp.float32)
+        return (values.T * lam_row[u, 0:1, begin : begin + count]).astype(jnp.bfloat16)
 
     def gradient(u, begin):
         at = turned(u)
-        pair = lam_pair[u]
+        pair = lam_pair[u] if u < direct else None
         for c in range(0, H, chunk):
             cols = slice(c, c + chunk)
             grad = jnp.dot(at, slope[u, :, cols], preferred_element_type=jnp.float32)
-            top = jnp.dot(pair, hid[u, :, cols], preferred_element_type=jnp.float32)
-            if begin:
-                w1g_ref[:, cols] = grad
-                wtot[:, cols] = top
-            else:
-                w1g_ref[:, cols] += grad
-                wtot[:, cols] += top
-
+            w1g_ref[:, cols] = grad if begin else w1g_ref[:, cols] + grad
+            if u < direct:
+                top = jnp.dot(pair, hid[u, :, cols], preferred_element_type=jnp.float32)
+                wtot[:, cols] = top if begin else wtot[:, cols] + top
+
+    w2g_ref[...] = jnp.zeros(w2g_ref.shape, jnp.float32)
     gradient(0, True)
-    relay(late)
-    step_forward(late - 1)
-    gradient(1, False)
-    behind = late + 1 - (ends - (T - 2 - late))
-    for u in range(2, late + 1 - behind):
+    left = list(range(1, ends))
+    for t in range(late, T - 1):
+        lead_relay(t)
+        step_forward(t)
+        if t < T - 2:
+            ready = [u for u in left if 2 * u <= t + 1]
+            for u in ready if t == T - 3 else ready[:2]:
+                gradient(u, False)
+                left.remove(u)
+    for u in left:
         gradient(u, False)
-
-    def full_step(t, carry):
-        relay(t)
-        step_forward(t - 1)
-        gradient(t - behind, False)
-        return carry
-
-    lax.fori_loop(late + 1, T - 2, full_step, 0)
-    relay(T - 2)
-    step_forward(T - 3)
-    relay(T - 1)
-    gradient(T - 2 - behind, False)
-    step_forward(T - 2)
-    pair_end[...] = lam_pair[ends]
+    w2g_ref[...] += jnp.sum(wtot[...], axis=0, keepdims=True)
+    lead_relay(T - 1)
     own_twin.wait_send()
     info_both.wait_send()
     lam_both.wait_send()
-    step_forward(T - 1)
-    at_end[...] = turned(ends)
+    at_end[:, 0:C] = turned(ends, 0, C)
+    twin_copy(T - 1, other).wait_recv()
+    at_end[:, C : 2 * C] = turned(ends, C, C)
+    forward(S + T - 1)
     sent = xs.at[pl.ds(0, T // 2)]
     remote(sent, sent, send_sem.at[0], ring_recv.at[0], twin_id).wait_send()
 
@@ -679,30 +737,30 @@
         pltpu.VMEM((slots // 2, 2 * C, H), bf16),
         pltpu.VMEM((3, 1, C), jnp.int32),
         pltpu.VMEM((C, E), f32),
+        pltpu.VMEM((16, H), f32),
+        pltpu.VMEM((D, 3, 1, C), f32),
         pltpu.VMEM((D, 8, C), f32),
         pltpu.VMEM((D, 8, C), f32),
-        pltpu.VMEM((D, 8, C), f32),
-        pltpu.VMEM((L, 8, C), f32),
+        pltpu.VMEM((L, D, 1, C), f32),
         pltpu.VMEM((L, D, 8, C), f32),
         pltpu.VMEM((slots // 2, 8, 2 * C), f32),
         pltpu.VMEM((slots // 2, 16, 2 * C), bf16),
         dma((6,)), dma((T,)), dma((T,)), dma((2,)), dma((2,)), dma((2,)), dma((1,)),
         pltpu.SemaphoreType.REGULAR((stages,)),
+        pltpu.SemaphoreType.REGULAR((1,)),
     ]
     held = pl.pallas_call(
         functools.partial(ring_kernel, sizes),
         out_shape=(
             pltpu.VMEM((C, E), bf16),
             pltpu.VMEM((rows, H), f32),
-            pltpu.VMEM((16, H), f32),
+            pltpu.VMEM((1, H), f32),
             pltpu.VMEM((rows, 2 * C), bf16),
-            pltpu.VMEM((16, 2 * C), bf16),
-            pltpu.VMEM((2 * C, H), bf16),
             pltpu.VMEM((2 * C, H), bf16),
             pltpu.VMEM((1, H), f32),
         ),
         in_specs=[hbm] * 6,
-        out_specs=(vmem,) * 8,
+        out_specs=(vmem,) * 6,
         scratch_shapes=scratch,
         compiler_params=pltpu.CompilerParams(
             collective_id=0, has_side_effects=True, vmem_limit_bytes=56 * 1024 * 1024
@@ -715,28 +773,25 @@
             jax.ShapeDtypeStruct((rows, H), f32),
             jax.ShapeDtypeStruct((1, H), f32),
         ),
-        in_specs=[vmem] * 8,
+        in_specs=[vmem] * 6,
         out_specs=(hbm,) * 3,
-        scratch_shapes=[pltpu.VMEM((rows, H), f32), pltpu.VMEM((1, H), f32), dma((6,))],
+        scratch_shapes=[pltpu.VMEM((rows, H), f32), dma((2 + PARTS,))],
         compiler_params=pltpu.CompilerParams(vmem_limit_bytes=4 * 1024 * 1024),
     )(*held)
 
 
-def finish(
-    emb_grad, w1g, wtot, at, pair, slope, hid, w2, emb_out, w1g_out, w2g_out, w1g_end, w2g_end, sem
-):
+def finish(emb_grad, w1g, w2g, at, slope, w2, emb_out, w1g_out, w2g_out, w1g_end, sem):
     H = w2.shape[1]
-    parts = 4
+    parts = PARTS
     wide = H // parts
-    copies = [pltpu.make_async_copy(emb_grad, emb_out, sem.at[0])]
-    copies[0].start()
+    copies = [
+        pltpu.make_async_copy(emb_grad, emb_out, sem.at[0]),
+        pltpu.make_async_copy(w2g, w2g_out, sem.at[1]),
+    ]
+    for copy in copies:
+        copy.start()
     for c in range(parts):
         cols = slice(c * wide, (c + 1) * wide)
-        if c == parts - 1:
-            top = wtot[...] + jnp.dot(pair[...], hid[...], preferred_element_type=jnp.float32)
-            w2g_end[...] = jnp.sum(top, axis=0, keepdims=True)
-            copies.append(pltpu.make_async_copy(w2g_end, w2g_out, sem.at[1]))
-            copies[-1].start()
         grad = jnp.dot(at[...], slope[:, cols], preferred_element_type=jnp.float32)
         w1g_end[:, cols] = (w1g[:, cols] + grad) * w2[:, cols]
         copies.append(

time: 28.9 us -> 28.4 us (0.983); the launches traced: 28.8 us -> 27.8 us
  Pallas kernels: 28.1 us -> 27.2 us
    pallas_call x1, Pallas kernels: 26.9 us -> 25.9 us  [ring_call(): pl.pallas_call(functools.partial(ring_kernel, sizes), out_shape=(pltpu.VM...]
where the time goes in v4:
time: 28.4 us; the launch traced here: 27.8 us
  Pallas kernels  27.2 us (96%)
  between operations  0.64 us (2%)
    pallas_call x1, Pallas kernels, ring_call(): pl.pallas_call(functools.partial(ring_kernel, sizes), out_shape=(pltpu.VM...  25.9 us
    pallas_call x1, Pallas kernels, ring_call(): pl.pallas_call(finish, out_shape=(jax.ShapeDtypeStruct((C, E), bf16), jax...  1.26 us

profile of v4, /device:TPU:0, one launch (start us, length us, event | category | flops | bytes accessed | tf_op | source)
XLA Modules:
  0.0 27.8 jit_solution(3012322816669162994)
XLA Ops:
  0.6 25.9 %shard_map.85 = (bf16[128,1024]{1,0:T(8,128)(2,1)S(1)}, f32[256,1024]{1,0:T(8,128)S(1)}, f32[1,1024]{1,0:T(1,128)S(1)}, bf16[256,256]{1,0:T(8,128)(2,1)S(1)}, bf...) custom-call(bf16[128,1024]{1,0:T(8,128)(2,1)} %emb_hbm.1, bf16[1024,1024]{1,0:T(8,128)(2,1)} %w1_hbm.1, ...), custom_call_target="tpu_custom_call" | custom-call | tf_op jit(solution)/shard_map/pallas_call | solution.py:752
  26.6 1.3 %shard_map.86 = (bf16[128,1024]{1,0:T(8,128)(2,1)}, f32[256,1024]{1,0:T(8,128)}, f32[1,1024]{1,0:T(1,128)}) custom-call(bf16[128,1024]{1,0:T(8,128)(2,1)S(1)} %get-tuple-element.12.emb_grad, f32[256,1024]{1,0:T(8,128)S(1)} %get-tuple-element.13.w1g, f32[1,1024]{1,0:T(1,128)S(1)} %get-tuple-element.14.w2g, bf16[256,256]{1,0:T(8,128)(2,1)S(1)} %get-tuple-element.15.at, ...), custom_call_target="tpu_custom_call" | custom-call | tf_op jit(solution)/shard_map/pallas_call | solution.py:769

commit v5 on v4

--- a/solution.py
+++ b/solution.py
@@ -361,8 +361,7 @@
         return lax.div(slot, 2), pl.multiple_of(lax.rem(slot, 2) * C, C)
 
     def block(slot):
-        u, row = spot(slot)
-        return xs.at[u, pl.ds(row, C)]
+        return xs.at[pl.ds(pl.multiple_of(slot * C, C), C)]
 
     load_e = pltpu.make_async_copy(emb_hbm, block(s), load_sem.at[0])
     load_w = pltpu.make_async_copy(w1_hbm, w1v, load_sem.at[1])
@@ -372,6 +371,7 @@
         pltpu.make_async_copy(labels_hbm, small.at[2], load_sem.at[4]),
         pltpu.make_async_copy(w2_hbm, w2v, load_sem.at[5]),
     ]
+    load_e.start()
     barrier = pltpu.get_barrier_semaphore()
 
     def flows(act):
@@ -392,7 +392,6 @@
     def _():
         hello_up((behind_id,), (ahead_id,))
 
-    load_e.start()
     load_w.start()
     for copy in load_small:
         copy.start()
@@ -481,16 +480,12 @@
 
     def forward(slot):
         u, row = spot(slot)
-        act = jnp.dot(xs[u, pl.ds(row, C), :], w1v[...], preferred_element_type=jnp.float32)
+        act = jnp.dot(block(slot)[...], w1v[...], preferred_element_type=jnp.float32)
         sg = 0.5 + 0.5 * jnp.tanh(0.5 * act)
         hidden = act * sg
         bend = sg + hidden * (1.0 - sg)
-        known = isinstance(slot, int)
-        if known and slot // 2 == ends:
-            slope_end[pl.ds(slot % 2 * C, C), :] = bend.astype(jnp.bfloat16)
-        else:
-            slope[u, pl.ds(row, C), :] = bend.astype(jnp.bfloat16)
-        if known and slot // 2 >= direct:
+        slope[u, pl.ds(row, C), :] = bend.astype(jnp.bfloat16)
+        if isinstance(slot, int) and slot // 2 >= direct:
             column = across(lam_row[slot // 2, 0:1, slot % 2 * C : slot % 2 * C + C], C)[:, 0:1]
             w2g_ref[...] += jnp.sum(hidden * column, axis=0, keepdims=True)
         else:
@@ -545,7 +540,15 @@
             ahead_copy(part(S + t, s, 0), t + P).start()
             behind_copy(part(S + t, s, 1), t + P).start()
 
-        twin_copy(t, s).start()
+        @pl.when((s == 0) & (t == T - 1 - P))
+        def _():
+            for way, peer in ((0, ahead_id), (1, behind_id)):
+                remote(
+                    part(S + t, 0, way), part(S + T - 1, 0, way), send_sem.at[0],
+                    twin_recv.at[T - 1], {**peer, "sub": other},
+                ).start()
+
+        pl.when((s > 0) | (t < T - 1))(lambda: twin_copy(t, s).start())
 
     def lead_relay(t):
         q = t + LEAD * s
@@ -553,6 +556,23 @@
             relay(q)
         else:
             pl.when(q < T)(lambda: relay(q))
+
+    half = 2 * PR
+
+    def lane_forward(lane_s):
+        spots = [(S + t) * C + lane_s * half for t in (T - 2, T - 1)]
+        x = jnp.concatenate([xs[pl.ds(spot, half), :] for spot in spots], axis=0)
+        act = jnp.dot(x, w1v[...], preferred_element_type=jnp.float32)
+        sg = 0.5 + 0.5 * jnp.tanh(0.5 * act)
+        hidden = act * sg
+        bend = (sg + hidden * (1.0 - sg)).astype(jnp.bfloat16)
+        for k in range(2):
+            here = slice(k * half, (k + 1) * half)
+            begin = k * C + lane_s * half
+            slope_end[begin : begin + half, :] = bend[here, :]
+            column = across(lam_row[ends, 0:1, k * C : k * C + C], C)
+            column = column[lane_s * half : (lane_s + 1) * half, 0:1]
+            w2g_ref[...] += jnp.sum(hidden[here, :] * column, axis=0, keepdims=True)
 
     def step_forward(t):
         twin_copy(t, other).wait_recv()
@@ -679,7 +699,7 @@
     chunk = min(H, 256)
 
     def turned(u, begin=0, count=2 * C):
-        values = xs[u, begin : begin + count, pl.ds(first, rows)].astype(jnp.float32)
+        values = xs[pl.ds(u * 2 * C + begin, count), pl.ds(first, rows)].astype(jnp.float32)
         return (values.T * lam_row[u, 0:1, begin : begin + count]).astype(jnp.bfloat16)
 
     def gradient(u, begin):
@@ -695,27 +715,41 @@
 
     w2g_ref[...] = jnp.zeros(w2g_ref.shape, jnp.float32)
     gradient(0, True)
-    left = list(range(1, ends))
-    for t in range(late, T - 1):
-        lead_relay(t)
+    gradient(1, False)
+    left = list(range(2, ends))
+    for t in range(late, T - 2):
+        if t < T - 4:
+            lead_relay(t)
+        else:
+            pl.when(s == 0)(lambda t=t: relay(t))
+        if t == T - 3:
+            pl.when(s > 0)(lambda: lane_forward(1))
         step_forward(t)
-        if t < T - 2:
-            ready = [u for u in left if 2 * u <= t + 1]
-            for u in ready if t == T - 3 else ready[:2]:
-                gradient(u, False)
-                left.remove(u)
-    for u in left:
-        gradient(u, False)
+        if t == T - 4:
+            pl.when(s > 0)(lambda: relay(T - 2))
+        ready = [u for u in left if 2 * u <= t + 1]
+        for u in ready if t == T - 3 else ready[:2]:
+            gradient(u, False)
+            left.remove(u)
+        if t == T - 4:
+            pl.when(s > 0)(lambda: relay(T - 1))
     w2g_ref[...] += jnp.sum(wtot[...], axis=0, keepdims=True)
-    lead_relay(T - 1)
+
+    @pl.when(s == 0)
+    def _():
+        relay(T - 2)
+        relay(T - 1)
+        lane_forward(0)
+
     own_twin.wait_send()
     info_both.wait_send()
     lam_both.wait_send()
-    at_end[:, 0:C] = turned(ends, 0, C)
-    twin_copy(T - 1, other).wait_recv()
-    at_end[:, C : 2 * C] = turned(ends, C, C)
-    forward(S + T - 1)
-    sent = xs.at[pl.ds(0, T // 2)]
+    for t in (T - 2, T - 1):
+        twin_copy(t, other).wait_recv()
+    at_end[...] = turned(ends)
+    pl.when(s == 0)(lambda: lane_forward(1))
+    pl.when(s > 0)(lambda: lane_forward(0))
+    sent = xs.at[pl.ds(0, T * 4 * PR)]
     remote(sent, sent, send_sem.at[0], ring_recv.at[0], twin_id).wait_send()
 
 
@@ -732,7 +766,7 @@
     stages = max(D - 1, crossing + 1) - 1
     scratch = [
         pltpu.VMEM((E, H), bf16),
-        pltpu.VMEM((slots // 2, 2 * C, E), bf16),
+        pltpu.VMEM((slots * C, E), bf16),
         pltpu.VMEM((slots // 2, 2 * C, H), bf16),
         pltpu.VMEM((slots // 2, 2 * C, H), bf16),
         pltpu.VMEM((3, 1, C), jnp.int32),
@@ -775,7 +809,7 @@
         ),
         in_specs=[vmem] * 6,
         out_specs=(hbm,) * 3,
-        scratch_shapes=[pltpu.VMEM((rows, H), f32), dma((2 + PARTS,))],
+        scratch_shapes=[pltpu.VMEM((rows, H), f32), dma((3,))],
         compiler_params=pltpu.CompilerParams(vmem_limit_bytes=4 * 1024 * 1024),
     )(*held)
 
@@ -794,12 +828,10 @@
         cols = slice(c * wide, (c + 1) * wide)
         grad = jnp.dot(at[...], slope[:, cols], preferred_element_type=jnp.float32)
         w1g_end[:, cols] = (w1g[:, cols] + grad) * w2[:, cols]
-        copies.append(
-            pltpu.make_async_copy(w1g_end.at[:, cols], w1g_out.at[:, cols], sem.at[2 + c])
-        )
-        copies[-1].start()
+        pltpu.make_async_copy(w1g_end.at[:, cols], w1g_out.at[:, cols], sem.at[2]).start()
     for copy in copies:
         copy.wait()
+    pltpu.make_async_copy(w1g_end, w1g_out, sem.at[2]).wait()
 
 
 def write_out(a_ref, b_ref, c_ref, a_out, b_out, c_out, sem):
@@ -881,7 +913,7 @@
     P = 2 * S
     held = D * L * C * (E + 2 * H) * 2
     gathers = (
-        M == 2 and S == 2 and D > 1 and C == LANES and rows % LANES == 0 and held <= 32 * 2**20
+        M == 2 and S == 2 and D > 3 and C == LANES and rows % LANES == 0 and held <= 32 * 2**20
     )
     if gathers:
         emb_grad, w1g, w2g = ring_call((D, M, S, C, E, H, rows, P), operands)

time: 28.4 us -> 28.1 us (0.989); the launches traced: 27.8 us -> 27.9 us
  no operation moved by 1% of the time
where the time goes in v5:
time: 28.1 us; the launch traced here: 27.9 us
  Pallas kernels  27.3 us (97%)
  between operations  0.64 us (2%)
    pallas_call x1, Pallas kernels, ring_call(): pl.pallas_call(functools.partial(ring_kernel, sizes), out_shape=(pltpu.VM...  26.1 us
    pallas_call x1, Pallas kernels, ring_call(): pl.pallas_call(finish, out_shape=(jax.ShapeDtypeStruct((C, E), bf16), jax...  1.23 us

profile of v5, /device:TPU:0, one launch (start us, length us, event | category | flops | bytes accessed | tf_op | source)
XLA Modules:
  0.0 27.9 jit_solution(9187465766005387922)
XLA Ops:
  0.6 26.1 %shard_map.85 = (bf16[128,1024]{1,0:T(8,128)(2,1)S(1)}, f32[256,1024]{1,0:T(8,128)S(1)}, f32[1,1024]{1,0:T(1,128)S(1)}, bf16[256,256]{1,0:T(8,128)(2,1)S(1)}, bf...) custom-call(bf16[128,1024]{1,0:T(8,128)(2,1)} %emb_hbm.1, bf16[1024,1024]{1,0:T(8,128)(2,1)} %w1_hbm.1, ...), custom_call_target="tpu_custom_call" | custom-call | tf_op jit(solution)/shard_map/pallas_call | solution.py:786
  26.7 1.2 %shard_map.86 = (bf16[128,1024]{1,0:T(8,128)(2,1)}, f32[256,1024]{1,0:T(8,128)}, f32[1,1024]{1,0:T(1,128)}) custom-call(bf16[128,1024]{1,0:T(8,128)(2,1)S(1)} %get-tuple-element.12.emb_grad, f32[256,1024]{1,0:T(8,128)S(1)} %get-tuple-element.13.w1g, f32[1,1024]{1,0:T(1,128)S(1)} %get-tuple-element.14.w2g, bf16[256,256]{1,0:T(8,128)(2,1)S(1)} %get-tuple-element.15.at, ...), custom_call_target="tpu_custom_call" | custom-call | tf_op jit(solution)/shard_map/pallas_call | solution.py:803

commit v6 on v5

--- a/solution.py
+++ b/solution.py
@@ -746,9 +746,17 @@
     lam_both.wait_send()
     for t in (T - 2, T - 1):
         twin_copy(t, other).wait_recv()
-    at_end[...] = turned(ends)
-    pl.when(s == 0)(lambda: lane_forward(1))
-    pl.when(s > 0)(lambda: lane_forward(0))
+
+    @pl.when(s == 0)
+    def _():
+        at_end[...] = turned(ends)
+        lane_forward(1)
+
+    @pl.when(s > 0)
+    def _():
+        at_end[...] = turned(ends)
+        lane_forward(0)
+
     sent = xs.at[pl.ds(0, T * 4 * PR)]
     remote(sent, sent, send_sem.at[0], ring_recv.at[0], twin_id).wait_send()
 

time: 28.1 us -> 28 us (level)
  no operation moved by 1% of the time
where the time goes in v6:
time: 28 us; the launch traced here: 27.8 us
  Pallas kernels  27.2 us (97%)
  between operations  0.64 us (2%)
    pallas_call x1, Pallas kernels, ring_call(): pl.pallas_call(functools.partial(ring_kernel, sizes), out_shape=(pltpu.VM...  26 us
    pallas_call x1, Pallas kernels, ring_call(): pl.pallas_call(finish, out_shape=(jax.ShapeDtypeStruct((C, E), bf16), jax...  1.23 us

profile of v6, /device:TPU:0, one launch (start us, length us, event | category | flops | bytes accessed | tf_op | source)
XLA Modules:
  0.0 27.8 jit_solution(13862317568946595338)
XLA Ops:
  0.6 26.0 %shard_map.85 = (bf16[128,1024]{1,0:T(8,128)(2,1)S(1)}, f32[256,1024]{1,0:T(8,128)S(1)}, f32[1,1024]{1,0:T(1,128)S(1)}, bf16[256,256]{1,0:T(8,128)(2,1)S(1)}, bf...) custom-call(bf16[128,1024]{1,0:T(8,128)(2,1)} %emb_hbm.1, bf16[1024,1024]{1,0:T(8,128)(2,1)} %w1_hbm.1, ...), custom_call_target="tpu_custom_call" | custom-call | tf_op jit(solution)/shard_map/pallas_call | solution.py:794
  26.6 1.2 %shard_map.86 = (bf16[128,1024]{1,0:T(8,128)(2,1)}, f32[256,1024]{1,0:T(8,128)}, f32[1,1024]{1,0:T(1,128)}) custom-call(bf16[128,1024]{1,0:T(8,128)(2,1)S(1)} %get-tuple-element.12.emb_grad, f32[256,1024]{1,0:T(8,128)S(1)} %get-tuple-element.13.w1g, f32[1,1024]{1,0:T(1,128)S(1)} %get-tuple-element.14.w2g, bf16[256,256]{1,0:T(8,128)(2,1)S(1)} %get-tuple-element.15.at, ...), custom_call_target="tpu_custom_call" | custom-call | tf_op jit(solution)/shard_map/pallas_call | solution.py:811
